TPU v7x, 32 devices: a whole 2x2x4 slice. The times are simulated.
32 devices in a mesh: dp: 2 (over core), wide: 4 (over y, x), narrow: 4 (over z).
Axes of the slice: x: 2, y: 2, z: 4, core: 2. Of those that a mesh axis runs over, the one named last changes fastest.
Arguments:
- block_input: float32 [1600, 4096], P('wide', ('dp', 'narrow')), as said below
- block_cotangent: float32 [1600, 4096], P('wide', ('dp', 'narrow')), may hold values from -6 to 6
- seq_start: int32 [32, 128], P(('dp', 'wide', 'narrow')), may hold values from 0 to 127, as said below
- ln1_gain: float32 [1600], P('wide'), may hold values from 0.5 to 1.5
- ln1_shift: float32 [1600], P('wide'), may hold values from -2 to 2
- w_qkv: float32 [1600, 3, 1600], P('wide', None, 'narrow'), may hold values from -0.15625 to 0.15625
- b_qv: float32 [2, 1600], P(None, 'narrow'), may hold values from -3 to 3
- w_out: float32 [1600, 1600], P('wide', 'narrow'), may hold values from -0.4375 to 0.4375
- b_out: float32 [1600], P('wide'), may hold values from -2 to 2
- ln2_gain: float32 [1600], P('wide'), may hold values from 0.5 to 1.5
- ln2_shift: float32 [1600], P('wide'), may hold values from -2 to 2
- w_fc: float32 [1600, 6400], P('wide', 'narrow'), may hold values from -0.15625 to 0.15625
- b_fc: float32 [6400], P('narrow'), may hold values from -3 to 3
- w_proj: float32 [1600, 6400], P('wide', 'narrow'), may hold values from -0.078125 to 0.078125
- b_proj: float32 [1600], P('wide'), may hold values from -2 to 2
Outputs:
- block_output: float32 [1600, 4096], P('wide', ('dp', 'narrow'))
- input_grad: float32 [1600, 4096], P('wide', ('dp', 'narrow'))
- grad_ln1_gain: float32 [1600], P('wide')
- grad_ln1_shift: float32 [1600], P('wide')
- grad_w_qkv: float32 [1600, 3, 1600], P('wide', None, 'narrow')
- grad_b_qv: float32 [2, 1600], P(None, 'narrow')
- grad_w_out: float32 [1600, 1600], P('wide', 'narrow')
- grad_b_out: float32 [1600], P('wide')
- grad_ln2_gain: float32 [1600], P('wide')
- grad_ln2_shift: float32 [1600], P('wide')
- grad_w_fc: float32 [1600, 6400], P('wide', 'narrow')
- grad_b_fc: float32 [6400], P('narrow')
- grad_w_proj: float32 [1600, 6400], P('wide', 'narrow')
- grad_b_proj: float32 [1600], P('wide')
Inputs may be any that keep to these rules, and one draw needn't show every extreme that they name: `block_input`: token activations of order one, with scales that differ from token to token. `seq_start`: along each row the values never fall; each equals the token's own position at the first token of its sequence and the start of its sequence after it. Block 0 holds one sequence of 128 tokens; some block ends with a sequence of one token.
All inputs are finite; a program needn't handle non-finite values.
Results may differ from a plain program's by a relative error of at most 0.011.
Values may be sent and summed in bfloat16 or wider, within the bound.
A program may use at most 320 MiB of HBM per device.

v0:
```python
import math
import jax
import jax.numpy as jnp
from jax import lax
from jax.sharding import PartitionSpec as P

HEADS = 25
HEAD = 64
EPS = 1e-05
GELU_C = math.sqrt(2.0 / math.pi)


def gelu_value(pre_act):
    inner = GELU_C * (pre_act + 0.044715 * pre_act * pre_act * pre_act)
    return 0.5 * pre_act * (1.0 + jnp.tanh(inner))


def gelu_slope(pre_act):
    tanh_part = jnp.tanh(GELU_C * (pre_act + 0.044715 * pre_act * pre_act * pre_act))
    return 0.5 * (1.0 + tanh_part) + 0.5 * pre_act * (1.0 - tanh_part * tanh_part) * GELU_C * (
        1.0 + 3.0 * 0.044715 * pre_act * pre_act
    )


def row_totals(first_term, second_term):
    return lax.psum(
        (jnp.sum(first_term, axis=1, keepdims=True), jnp.sum(second_term, axis=1, keepdims=True)),
        "wide",
    )


def norm_forward(inputs, gain_shard, shift_shard):
    full_width = inputs.shape[1] * lax.axis_size("wide")
    total_sum, square_sum = row_totals(inputs, inputs * inputs)
    mean_row = total_sum / full_width
    inv_std = lax.rsqrt(square_sum / full_width - mean_row * mean_row + EPS)
    normed = (inputs - mean_row) * inv_std
    return (normed, inv_std, (normed * gain_shard + shift_shard).astype(jnp.bfloat16))


def norm_backward(row_grads, normed, inv_std, gain_shard):
    full_width = row_grads.shape[1] * lax.axis_size("wide")
    scaled = row_grads * gain_shard
    first_sum, second_sum = row_totals(scaled, scaled * normed)
    return inv_std * (scaled - first_sum / full_width - normed * (second_sum / full_width))


def gather_narrow(values):
    return lax.all_gather(values, "narrow", axis=0, tiled=True)


def sum_narrow(partial_value):
    return lax.psum_scatter(partial_value, "narrow", scatter_dimension=0, tiled=True)


def sum_wide(gathered, weight_bf, transposed):

    def partial_rows():
        if transposed:
            return lax.dot_general(
                gathered, weight_bf, (((1,), (1,)), ((), ())), preferred_element_type=jnp.float32
            )
        return jnp.dot(gathered, weight_bf, preferred_element_type=jnp.float32)

    return lax.psum_scatter(partial_rows(), "wide", scatter_dimension=0, tiled=True)


def project_wide(activations, weight_bf):
    return sum_narrow(
        jnp.dot(
            lax.all_gather(activations, "wide", axis=0, tiled=True),
            weight_bf,
            preferred_element_type=jnp.float32,
        )
    )


def fold_wide(grad_rows, inputs_all, weight_bf):
    block_rows = lax.all_gather(grad_rows, "wide", axis=0, tiled=True)
    weight_grad = lax.dot_general(
        inputs_all, block_rows, (((0,), (0,)), ((), ())), preferred_element_type=jnp.float32
    )
    back_rows = lax.dot_general(
        block_rows, weight_bf, (((1,), (1,)), ((), ())), preferred_element_type=jnp.float32
    )
    weight_grad, partial_value = (weight_grad, back_rows)
    return (weight_grad, sum_narrow(partial_value))


def weight_grad_block(activations, grads_all):
    return lax.dot_general(
        lax.all_gather(activations, "wide", axis=0, tiled=True),
        grads_all,
        (((0,), (0,)), ((), ())),
        preferred_element_type=jnp.float32,
    )


def to_heads(values):
    return lax.all_to_all(values, "narrow", split_axis=0, concat_axis=2, tiled=True)


def from_heads(values):
    return lax.all_to_all(values, "narrow", split_axis=2, concat_axis=0, tiled=True)


def block_mask(starts):
    position = jnp.arange(starts.shape[0])
    return (position[None, :] <= position[:, None]) & (starts[:, None] == starts[None, :])


def split_heads(values):
    return values.reshape(values.shape[0], HEADS, HEAD)


def attend_forward(heads_all, allowed):
    score_scale = 1.0 / math.sqrt(HEAD)
    queries = split_heads(heads_all[:, 0])
    keys_part = split_heads(heads_all[:, 1])
    values_part = split_heads(heads_all[:, 2])
    scores = (
        jnp.einsum("ihd,jhd->hij", queries, keys_part, preferred_element_type=jnp.float32)
        * score_scale
    )
    log_total = jnp.log(jnp.sum(jnp.where(allowed, jnp.exp(scores), 0.0), axis=2, keepdims=True))
    attn_probs = jnp.where(allowed, jnp.exp(scores - log_total), 0.0).astype(jnp.bfloat16)
    attended = jnp.einsum(
        "hij,jhd->ihd", attn_probs, values_part, preferred_element_type=jnp.float32
    )
    return (attended.reshape(heads_all.shape[0], HEADS * HEAD).astype(jnp.bfloat16), log_total)


def attend_backward(heads_all, allowed, log_total, attended_cot):
    score_scale = 1.0 / math.sqrt(HEAD)
    queries = split_heads(heads_all[:, 0])
    keys_part = split_heads(heads_all[:, 1])
    values_part = split_heads(heads_all[:, 2])
    scores = (
        jnp.einsum("ihd,jhd->hij", queries, keys_part, preferred_element_type=jnp.float32)
        * score_scale
    )
    probs_full = jnp.where(allowed, jnp.exp(scores - log_total), 0.0)
    cot_heads = split_heads(attended_cot)
    dprobs = jnp.einsum("ihd,jhd->hij", cot_heads, values_part, preferred_element_type=jnp.float32)
    row_delta = jnp.sum(probs_full * dprobs, axis=2, keepdims=True)
    score_cot = (probs_full * (dprobs - row_delta) * score_scale).astype(jnp.bfloat16)
    query_grad = jnp.einsum(
        "hij,jhd->ihd", score_cot, keys_part, preferred_element_type=jnp.float32
    )
    key_grad = jnp.einsum("hij,ihd->jhd", score_cot, queries, preferred_element_type=jnp.float32)
    value_grad = jnp.einsum(
        "hij,ihd->jhd",
        probs_full.astype(jnp.bfloat16),
        cot_heads,
        preferred_element_type=jnp.float32,
    )
    stacked = jnp.stack([query_grad, key_grad, value_grad], axis=1)
    return stacked.reshape(heads_all.shape[0], 3, HEADS * HEAD)


def local(
    block_input,
    block_cotangent,
    seq_start,
    ln1_gain,
    ln1_shift,
    w_qkv,
    b_qv,
    w_out,
    b_out,
    ln2_gain,
    ln2_shift,
    w_fc,
    b_fc,
    w_proj,
    b_proj,
):
    narrow_count = lax.axis_size("narrow")
    narrow_index = lax.axis_index("narrow")
    part_width = w_qkv.shape[2]
    hidden_width = w_fc.shape[1]
    rows_input = block_input.T
    rows_cot = block_cotangent.T
    wq_bf = w_qkv.astype(jnp.bfloat16).reshape(w_qkv.shape[0], 3 * part_width)
    wo_bf = w_out.T.astype(jnp.bfloat16)
    wf_bf = w_fc.astype(jnp.bfloat16)
    wp_bf = w_proj.T.astype(jnp.bfloat16)
    bias_three = jnp.stack([b_qv[0], jnp.zeros_like(b_qv[0]), b_qv[1]])
    normed_one, inv_one, norm_one = norm_forward(rows_input, ln1_gain, ln1_shift)
    norm_one_all = gather_narrow(norm_one)
    qkv_rows = sum_wide(norm_one_all, wq_bf, False)
    grid_rows = qkv_rows.shape[0]
    qkv_grid = (qkv_rows.reshape(grid_rows, 3, part_width) + bias_three).astype(jnp.bfloat16)
    heads_all = to_heads(qkv_grid)
    block_rows = heads_all.shape[0]
    allowed = block_mask(seq_start[0])
    attended, log_total = attend_forward(heads_all, allowed)
    attended_grid = from_heads(attended.reshape(block_rows, 1, HEADS * HEAD)).reshape(
        grid_rows, part_width
    )
    residual = rows_input + project_wide(attended_grid, wo_bf) + b_out
    normed_two, inv_two, norm_two = norm_forward(residual, ln2_gain, ln2_shift)
    norm_two_all = gather_narrow(norm_two)
    pre_act = sum_wide(norm_two_all, wf_bf, False) + b_fc
    hidden = gelu_value(pre_act).astype(jnp.bfloat16)
    output_rows = residual + project_wide(hidden, wp_bf) + b_proj
    cot_rows = rows_cot.astype(jnp.bfloat16)
    cot_all = gather_narrow(cot_rows)
    grad_w_proj = weight_grad_block(hidden, cot_all)
    pre_grad = sum_wide(cot_all, wp_bf, True) * gelu_slope(pre_act)
    pre_cot = pre_grad.astype(jnp.bfloat16)
    grad_w_fc, norm_two_grad = fold_wide(pre_cot, norm_two_all, wf_bf)
    resid_grad = rows_cot + norm_backward(norm_two_grad, normed_two, inv_two, ln2_gain)
    resid_cot = resid_grad.astype(jnp.bfloat16)
    resid_all = gather_narrow(resid_cot)
    grad_w_out = weight_grad_block(attended_grid, resid_all)
    attended_cot = sum_wide(resid_all, wo_bf, True).astype(jnp.bfloat16)
    cot_heads = to_heads(attended_cot.reshape(grid_rows, 1, part_width)).reshape(
        block_rows, HEADS * HEAD
    )
    qkv_grad = attend_backward(heads_all, allowed, log_total, cot_heads)
    qkv_cot = from_heads(qkv_grad.astype(jnp.bfloat16))
    grad_w_qkv, norm_one_grad = fold_wide(
        qkv_cot.reshape(grid_rows, 3 * part_width), norm_one_all, wq_bf
    )
    grad_input_rows = resid_grad + norm_backward(norm_one_grad, normed_one, inv_one, ln1_gain)
    qkv_sums = jnp.sum(qkv_grad, axis=0)
    bias_qv_full = jnp.stack([qkv_sums[0], qkv_sums[2]])
    fc_full = jnp.zeros((narrow_count * hidden_width,), jnp.float32)
    fc_full = lax.dynamic_update_slice_in_dim(
        fc_full, jnp.sum(pre_grad, axis=0), narrow_index * hidden_width, 0
    )
    bias_qv_sum, fc_sum = lax.psum((bias_qv_full, fc_full), ("dp", "wide", "narrow"))
    grad_b_qv = lax.dynamic_slice_in_dim(bias_qv_sum, narrow_index * part_width, part_width, 1)
    grad_b_fc = lax.dynamic_slice_in_dim(fc_sum, narrow_index * hidden_width, hidden_width, 0)
    row_terms = (
        jnp.sum(norm_one_grad * normed_one, axis=0),
        jnp.sum(norm_one_grad, axis=0),
        jnp.sum(resid_grad, axis=0),
        jnp.sum(norm_two_grad * normed_two, axis=0),
        jnp.sum(norm_two_grad, axis=0),
        jnp.sum(rows_cot, axis=0),
    )
    gain_one_grad, shift_one_grad, out_bias_grad, gain_two_grad, shift_two_grad, proj_bias_grad = (
        lax.psum(
            (row_terms[0], row_terms[1], row_terms[2], row_terms[3], row_terms[4], row_terms[5]),
            ("dp", "narrow"),
        )
    )
    qkv_total, out_total, fc_total, proj_total = lax.psum(
        (grad_w_qkv.reshape(w_qkv.shape), grad_w_out.T, grad_w_fc, grad_w_proj.T), "dp"
    )
    return (
        output_rows.T,
        grad_input_rows.T,
        gain_one_grad,
        shift_one_grad,
        qkv_total,
        grad_b_qv,
        out_total,
        out_bias_grad,
        gain_two_grad,
        shift_two_grad,
        fc_total,
        grad_b_fc,
        proj_total,
        proj_bias_grad,
    )


def solution(mesh):
    return jax.shard_map(
        local,
        mesh=mesh,
        in_specs=(
            P("wide", ("dp", "narrow")),
            P("wide", ("dp", "narrow")),
            P(("dp", "wide", "narrow"), None),
            P("wide"),
            P("wide"),
            P("wide", None, "narrow"),
            P(None, "narrow"),
            P("wide", "narrow"),
            P("wide"),
            P("wide"),
            P("wide"),
            P("wide", "narrow"),
            P("narrow"),
            P("wide", "narrow"),
            P("wide"),
        ),
        out_specs=(
            P("wide", ("dp", "narrow")),
            P("wide", ("dp", "narrow")),
            P("wide"),
            P("wide"),
            P("wide", None, "narrow"),
            P(None, "narrow"),
            P("wide", "narrow"),
            P("wide"),
            P("wide"),
            P("wide"),
            P("wide", "narrow"),
            P("narrow"),
            P("wide", "narrow"),
            P("wide"),
        ),
        check_vma=False,
    )
```

profile of v0, /device:TPU:0, one launch (start us, length us, event | category | flops | bytes accessed | tf_op | source)
XLA Modules:
  0.0 1337.4 jit_solution(5024976810314251157)
XLA Ops:
  9.8 11.4 all-reduce.5
  25.0 34.8 %all-gather.9.cloned.1.call-done = bf16[2048,400]{0,1:T(8,128)(2,1)} async-done(((bf16[512,400]{0,1:T(8,128)(2,1)}), bf16[2048,400]{0,1:T(8,128)(2,1)}) %all-gather.9.cloned.1.call-update) | async-done | bytes 1638416 | tf_op jit(solution)/shard_map/all_gather | solution.py:49
  67.2 96.4 %reduce-scatter.9.cloned.1.call-done = f32[512,1200]{0,1:T(8,128)} async-done(((f32[2048,1200]{0,1:T(8,128)}), f32[512,1200]{0,1:T(8,128)}) %reduce-scatter.9.cloned.1.call-update) | async-done | bytes 2457616 | tf_op jit(solution)/shard_map/reduce_scatter | solution.py:65
  173.5 47.8 %all-to-all-done = bf16[512,3,400]{2,1,0:T(4,128)(2,1)S(1)} async-done(((bf16[512,3,400]{2,1,0:T(4,128)(2,1)}), bf16[512,3,400]{2,1,0:T(4,128)(2,1)S(1)}, u32[]{:S(2)}, u32[]{:S(2)}) %all-to-all-start) | async-done | bytes 1228832 | tf_op jit(solution)/shard_map/all_to_all | solution.py:100
  234.3 9.1 reduce.2
  243.5 14.0 %all_to_all.63 = bf16[4,2,25600]{2,1,0:T(2,128)(2,1)S(1)} all-to-all(bf16[4,2,25600]{2,1,0:T(2,128)(2,1)S(1)} %reshape.90), channel_id=1, replica_groups=mesh['dp'=2,'wide'=4,'narrow'=4] {'narrow'}, dimensions={0} | all-to-all | bytes 819200 | tf_op jit(solution)/shard_map/all_to_all | solution.py:104
  259.0 29.5 %all-gather.11.cloned.1.call-done = bf16[2048,400]{0,1:T(8,128)(2,1)} async-done(((bf16[512,400]{0,1:T(8,128)(2,1)}), bf16[2048,400]{0,1:T(8,128)(2,1)}) %all-gather.11.cloned.1.call-update) | async-done | bytes 1638416 | tf_op jit(solution)/shard_map/all_gather | solution.py:71
  294.6 60.6 %reduce-scatter.11.cloned.1.call-done = f32[512,400]{0,1:T(8,128)} async-done(((f32[2048,400]{0,1:T(8,128)}), f32[512,400]{0,1:T(8,128)}) %reduce-scatter.11.cloned.1.call-update) | async-done | bytes 819216 | tf_op jit(solution)/shard_map/reduce_scatter | solution.py:53
  356.6 9.8 all-reduce.4
  367.7 27.7 %all-gather.17.cloned.1.call-done = bf16[2048,400]{0,1:T(8,128)(2,1)} async-done(((bf16[512,400]{0,1:T(8,128)(2,1)}), bf16[2048,400]{0,1:T(8,128)(2,1)}) %all-gather.17.cloned.1.call-update) | async-done | bytes 1638416 | tf_op jit(solution)/shard_map/all_gather | solution.py:49
  395.4 10.6 fusion.34
  406.1 28.3 %all-gather.13.cloned.1.call-done = bf16[2048,400]{0,1:T(8,128)(2,1)} async-done(((bf16[512,400]{0,1:T(8,128)(2,1)}), bf16[2048,400]{0,1:T(8,128)(2,1)}) %all-gather.13.cloned.1.call-update) | async-done | bytes 1638416 | tf_op jit(solution)/shard_map/all_gather | solution.py:49
  434.3 11.3 fusion.40
  445.7 115.5 %reduce-scatter.17.cloned.1.call-done = f32[512,1600]{0,1:T(8,128)} async-done(((f32[2048,1600]{0,1:T(8,128)}), f32[512,1600]{0,1:T(8,128)}) %reduce-scatter.17.cloned.1.call-update) | async-done | bytes 3276816 | tf_op jit(solution)/shard_map/reduce_scatter | solution.py:65
  561.2 128.0 %reduce-scatter.13.cloned.1.call-done = f32[512,1600]{0,1:T(8,128)} async-done(((f32[2048,1600]{0,1:T(8,128)}), f32[512,1600]{0,1:T(8,128)}) %reduce-scatter.13.cloned.1.call-update) | async-done | bytes 3276816 | tf_op jit(solution)/shard_map/reduce_scatter | solution.py:65
  695.8 71.6 %all-gather.19.cloned.1.call-done = bf16[2048,1600]{0,1:T(8,128)(2,1)} async-done(((bf16[512,1600]{0,1:T(8,128)(2,1)}), bf16[2048,1600]{0,1:T(8,128)(2,1)}) %all-gather.19.cloned.1.call-update) | async-done | bytes 6553616 | tf_op jit(solution)/shard_map/all_gather | solution.py:79
  767.4 8.5 fusion.38
  776.4 65.4 %all-gather.15.cloned.1.call-done = bf16[2048,1600]{0,1:T(8,128)(2,1)} async-done(((bf16[512,1600]{0,1:T(8,128)(2,1)}), bf16[2048,1600]{0,1:T(8,128)(2,1)}) %all-gather.15.cloned.1.call-update) | async-done | bytes 6553616 | tf_op jit(solution)/shard_map/all_gather | solution.py:71
  841.8 8.5 fusion.36
  850.3 56.2 %reduce-scatter.19.cloned.1.call-done = f32[512,400]{0,1:T(8,128)} async-done(((f32[2048,400]{0,1:T(8,128)}), f32[512,400]{0,1:T(8,128)}) %reduce-scatter.19.cloned.1.call-update) | async-done | bytes 819216 | tf_op jit(solution)/shard_map/reduce_scatter | solution.py:53
  908.1 9.9 all-reduce.3
  917.9 53.2 %reduce-scatter.15.cloned.1.call-done = f32[512,400]{0,1:T(8,128)} async-done(((f32[2048,400]{0,1:T(8,128)}), f32[512,400]{0,1:T(8,128)}) %reduce-scatter.15.cloned.1.call-update) | async-done | bytes 819216 | tf_op jit(solution)/shard_map/reduce_scatter | solution.py:53
  975.5 38.2 %all-gather.21.cloned.1.call-done = bf16[2048,400]{0,1:T(8,128)(2,1)} async-done(((bf16[512,400]{0,1:T(8,128)(2,1)}), bf16[2048,400]{0,1:T(8,128)(2,1)}) %all-gather.21.cloned.1.call-update) | async-done | bytes 1638416 | tf_op jit(solution)/shard_map/all_gather | solution.py:49
  1017.9 44.0 %reduce-scatter.21.cloned.1.call-done = f32[512,400]{0,1:T(8,128)} async-done(((f32[2048,400]{0,1:T(8,128)}), f32[512,400]{0,1:T(8,128)}) %reduce-scatter.21.cloned.1.call-update) | async-done | bytes 819216 | tf_op jit(solution)/shard_map/reduce_scatter | solution.py:65
  1074.5 9.7 all-to-all-done.2
  1103.1 40.4 %all_to_all.64 = bf16[128,3,1600]{0,1,2:T(4,128)(2,1)S(1)} all-to-all(bf16[128,3,1600]{0,1,2:T(4,128)(2,1)S(1)} %fusion.9), channel_id=1, replica_groups=mesh['dp'=2,'wide'=4,'narrow'=4] {'narrow'}, dimensions={2} | all-to-all | bytes 2457600 | tf_op jit(solution)/shard_map/all_to_all | solution.py:104
  1145.6 56.5 %all-gather.23.cloned.1.call-done = bf16[2048,1200]{0,1:T(8,128)(2,1)} async-done(((bf16[512,1200]{0,1:T(8,128)(2,1)}), bf16[2048,1200]{0,1:T(8,128)(2,1)}) %all-gather.23.cloned.1.call-update) | async-done | bytes 4915216 | tf_op jit(solution)/shard_map/all_gather | solution.py:79
  1209.0 8.2 fusion.88
  1217.2 7.7 convolution_bitcast_fusion
  1237.0 42.9 %all-reduce = (f32[2,1600]{1,0:T(2,128)S(1)}, f32[6400]{0:T(1024)S(1)}) all-reduce(f32[2,1600]{1,0:T(2,128)S(1)} %pad_maximum_fusion.1, f32[6400]{0:T(1024)S(1)} %dynamic_update_slice.3), channel_id=1, replica_groups=mesh['dp'=2,'wide'=4,'narrow'=4] {'dp','wide','narrow'}, use_global_device_ids=true, to_apply=%region_32.33 | all-reduce | flops 9600 | bytes 76800 | tf_op jit(solution)/shard_map/psum | solution.py:233
  1283.1 9.7 all-reduce.2
  1292.8 28.2 %all-reduce.1 = (f32[400]{0:T(512)}, f32[400]{0:T(512)}, f32[400]{0:T(512)}, f32[400]{0:T(512)}, f32[400]{0:T(512)}, /*index=5*/f32[400]{0:T(512)}) all-reduce(f32[400]{0:T(512)S(1)} %get-tuple-element.114, f32[400]{0:T(512)S(1)} %get-tuple-element.119, ...), channel_id=1, replica_groups=mesh['dp'=2,'wide'=4,'narrow'=4] {'dp','narrow'}, use_global_device_ids=true, to_apply=%region_27.28 | all-reduce | flops 2400 | bytes 19200 | tf_op jit(solution)/shard_map/psum | solution.py:245
  (177 shorter events, 129.1 us)
Async XLA Ops:
  7.2 14.0 %copy-start = (f32[400,512]{1,0:T(8,128)S(1)}, f32[400,512]{1,0:T(8,128)}, u32[]{:S(2)}) copy-start(f32[400,512]{1,0:T(8,128)} %param.15) | copy-start | bytes 2457604
  7.2 14.0 %copy-start.20 = (f32[400]{0:T(512)S(1)}, f32[400]{0:T(512)}, u32[]{:S(2)}) copy-start(f32[400]{0:T(512)} %param.18) | copy-start | bytes 4804
  7.2 14.0 %copy-start.24 = (f32[400]{0:T(512)S(1)}, f32[400]{0:T(512)}, u32[]{:S(2)}) copy-start(f32[400]{0:T(512)} %param.19) | copy-start | bytes 4804
  7.2 52.6 %all-gather.9.cloned.1.call-start = ((), (), s32[]{:S(2)}) async-start(), calls=%async_computation.12 | async-start | bytes 2048000 | tf_op jit(solution)/shard_map/all_gather | solution.py:49
  22.2 141.4 %reduce-scatter.9.cloned.1.call-start = ((), (), s32[]{:S(2)}) async-start(), calls=%async_computation.13 | async-start | bytes 12288000 | tf_op jit(solution)/shard_map/reduce_scatter | solution.py:65
  24.9 41.5 %copy-start.17 = (bf16[400,3,400]{0,2,1:T(8,128)(2,1)}, bf16[400,3,400]{0,2,1:T(8,128)(2,1)S(1)}, u32[]{:S(2)}) copy-start(bf16[400,3,400]{0,2,1:T(8,128)(2,1)S(1)} %copy.134) | copy-start | bytes 2880004
  168.5 52.7 %all-to-all-start = ((bf16[512,3,400]{2,1,0:T(4,128)(2,1)}), bf16[512,3,400]{2,1,0:T(4,128)(2,1)S(1)}, u32[]{:S(2)}, u32[]{:S(2)}) async-start(bf16[512,3,400]{2,1,0:T(4,128)(2,1)} %copy.135), calls=%async_computation.1 | async-start | bytes 4194304 | tf_op jit(solution)/shard_map/all_to_all | solution.py:100
  173.2 115.3 %all-gather.11.cloned.1.call-start = ((), (), s32[]{:S(2)}) async-start(), calls=%async_computation.14 | async-start | bytes 2048000 | tf_op jit(solution)/shard_map/all_gather | solution.py:71
  257.9 30.6 %copy-start.2 = (f32[400,400]{1,0:T(8,128)S(1)}, f32[400,400]{1,0:T(8,128)}, u32[]{:S(2)}) copy-start(f32[400,400]{1,0:T(8,128)} %param.22) | copy-start | bytes 1920004
  258.9 96.3 %reduce-scatter.11.cloned.1.call-start = ((), (), s32[]{:S(2)}) async-start(), calls=%async_computation.15 | async-start | bytes 4096000 | tf_op jit(solution)/shard_map/reduce_scatter | solution.py:53
  292.6 62.6 %copy-start.28 = (f32[400]{0:T(512)S(1)}, f32[400]{0:T(512)}, u32[]{:S(2)}) copy-start(f32[400]{0:T(512)} %param.23) | copy-start | bytes 4804
  292.7 102.7 %all-gather.17.cloned.1.call-start = ((), (), s32[]{:S(2)}) async-start(), calls=%async_computation.20 | async-start | bytes 2048000 | tf_op jit(solution)/shard_map/all_gather | solution.py:49
  294.6 71.9 %copy-start.19 = (f32[400]{0:T(512)S(1)}, f32[400]{0:T(512)}, u32[]{:S(2)}) copy-start(f32[400]{0:T(512)} %param.24) | copy-start | bytes 4804
  294.6 71.9 %copy-start.25 = (f32[400]{0:T(512)S(1)}, f32[400]{0:T(512)}, u32[]{:S(2)}) copy-start(f32[400]{0:T(512)} %param.25) | copy-start | bytes 4804
  294.6 139.8 %all-gather.13.cloned.1.call-start = ((), (), s32[]{:S(2)}) async-start(), calls=%async_computation.16 | async-start | bytes 2048000 | tf_op jit(solution)/shard_map/all_gather | solution.py:49
  367.4 193.8 %reduce-scatter.17.cloned.1.call-start = ((), (), s32[]{:S(2)}) async-start(), calls=%async_computation.21 | async-start | bytes 16384000 | tf_op jit(solution)/shard_map/reduce_scatter | solution.py:65
  406.0 283.3 %reduce-scatter.13.cloned.1.call-start = ((), (), s32[]{:S(2)}) async-start(), calls=%async_computation.17 | async-start | bytes 16384000 | tf_op jit(solution)/shard_map/reduce_scatter | solution.py:65
  445.6 243.7 %copy-start.21 = (f32[1600]{0:T(1024)S(1)}, f32[1600]{0:T(1024)}, u32[]{:S(2)}) copy-start(f32[1600]{0:T(1024)} %param.27) | copy-start | bytes 19204
  445.6 321.8 %all-gather.19.cloned.1.call-start = ((), (), s32[]{:S(2)}) async-start(), calls=%async_computation.22 | async-start | bytes 8192000 | tf_op jit(solution)/shard_map/all_gather | solution.py:79
  695.2 146.6 %all-gather.15.cloned.1.call-start = ((), (), s32[]{:S(2)}) async-start(), calls=%async_computation.18 | async-start | bytes 8192000 | tf_op jit(solution)/shard_map/all_gather | solution.py:71
  695.8 210.8 %reduce-scatter.19.cloned.1.call-start = ((), (), s32[]{:S(2)}) async-start(), calls=%async_computation.23 | async-start | bytes 4096000 | tf_op jit(solution)/shard_map/reduce_scatter | solution.py:53
  775.9 195.3 %reduce-scatter.15.cloned.1.call-start = ((), (), s32[]{:S(2)}) async-start(), calls=%async_computation.19 | async-start | bytes 4096000 | tf_op jit(solution)/shard_map/reduce_scatter | solution.py:53
  850.3 120.9 %copy-start.26 = (f32[400]{0:T(512)S(1)}, f32[400]{0:T(512)}, u32[]{:S(2)}) copy-start(f32[400]{0:T(512)} %param.29) | copy-start | bytes 4804
  850.3 163.4 %all-gather.21.cloned.1.call-start = ((), (), s32[]{:S(2)}) async-start(), calls=%async_computation.24 | async-start | bytes 2048000 | tf_op jit(solution)/shard_map/all_gather | solution.py:49
  975.5 86.4 %reduce-scatter.21.cloned.1.call-start = ((), (), s32[]{:S(2)}) async-start(), calls=%async_computation.25 | async-start | bytes 4096000 | tf_op jit(solution)/shard_map/reduce_scatter | solution.py:65
  1067.7 16.5 %all-to-all-start.2 = ((bf16[4,2,25600]{2,1,0:T(2,128)(2,1)}), bf16[4,2,25600]{2,1,0:T(2,128)(2,1)S(1)}, u32[]{:S(2)}, u32[]{:S(2)}) async-start(bf16[4,2,25600]{2,1,0:T(2,128)(2,1)} %reshape.92), calls=%async_computation.9 | async-start | bytes 819200 | tf_op jit(solution)/shard_map/all_to_all | solution.py:100
  1072.4 129.8 %all-gather.23.cloned.1.call-start = ((), (), s32[]{:S(2)}) async-start(), calls=%async_computation.26 | async-start | bytes 6144000 | tf_op jit(solution)/shard_map/all_gather | solution.py:79
  1145.4 135.8 %reduce-scatter.23.cloned.1.call-start = ((), (), s32[]{:S(2)}) async-start(), calls=%async_computation.27 | async-start | bytes 4096000 | tf_op jit(solution)/shard_map/reduce_scatter | solution.py:53
  1208.9 113.3 %all-reduce.9.cloned.1.call-start = ((), (), s32[]{:S(2)}) async-start(), calls=%async_computation.28 | async-start | bytes 17203200 | tf_op jit(solution)/shard_map/psum | solution.py:250
  1209.0 17.8 %slice-start = ((s8[4915200]{0:T(1024)(128)(4,1)}), s8[720896]{0:T(1024)(128)(4,1)S(1)}, s32[]{:S(2)}) async-start(s8[4915200]{0:T(1024)(128)(4,1)} %bitcast.192), calls=%async_computation.29 | async-start | bytes 1441792
  1236.3 56.5 %copy-start.22 = (f32[400]{0:T(512)S(1)}, f32[400]{0:T(512)}, u32[]{:S(2)}) copy-start(f32[400]{0:T(512)} %get-tuple-element.144) | copy-start | bytes 4804
  1281.2 39.8 %copy-start.3 = (f32[512,400]{0,1:T(8,128)S(1)}, f32[512,400]{0,1:T(8,128)}, u32[]{:S(2)}) copy-start(f32[512,400]{0,1:T(8,128)} %reduce-scatter.23.cloned.1.call-done) | copy-start | bytes 2457604
  (20 other events, 80.6 us)
Sparse Core Ops, SparseCore 0:
  22.3 37.4 all-gather.8
  66.6 96.9 reduce-scatter.8
  259.1 29.3 all-gather.10
  292.8 62.4 reduce-scatter.10
  357.2 38.0 all-gather.16
  397.3 36.9 all-gather.12
  437.5 123.7 reduce-scatter.16
  564.4 124.8 reduce-scatter.12
  695.3 72.0 all-gather.18
  769.7 72.0 all-gather.14
  844.1 62.4 reduce-scatter.18
  908.7 62.4 reduce-scatter.14
  975.6 38.0 all-gather.20
  1018.0 43.8 reduce-scatter.20
  1145.5 56.5 all-gather.22
  1209.0 63.3 reduce-scatter.22
  1276.3 38.5 all-reduce.8
where the time goes:
time: 1340 us
  waiting for transfers between devices  964 us (72%)
  blocking collectives  166 us (12%)
  matrix products  98.5 us (7%)
  other arithmetic  45.2 us (3%)
  local copies, waits for them, and re-layouts  37.6 us (3%)
  between operations  14.7 us (1%)
    reduce_scatter x4, waiting for transfers between devices, sum_wide(): lax.psum_scatter(partial_rows(), 'wide', scatter_dimension=0, tiled=True)  384 us
    reduce_scatter x4, waiting for transfers between devices, sum_narrow(): lax.psum_scatter(partial_value, 'narrow', scatter_dimension=0, tiled=True)  170 us
    all_gather x4, waiting for transfers between devices, gather_narrow(): return lax.all_gather(values, 'narrow', axis=0, tiled=True)  129 us
    all_gather x2, waiting for transfers between devices, fold_wide(): block_rows = lax.all_gather(grad_rows, 'wide', axis=0, tiled=True)  128 us
    all_gather x2, waiting for transfers between devices, project_wide(): lax.all_gather(activations, 'wide', axis=0, tiled=True)  94.9 us
    all_to_all x2, waiting for transfers between devices, to_heads(): lax.all_to_all(values, 'narrow', split_axis=0, concat_axis=2, tiled=True)  57.5 us
    all_to_all x2, blocking collectives, from_heads(): lax.all_to_all(values, 'narrow', split_axis=2, concat_axis=0, tiled=True)  54.3 us
    psum x1, blocking collectives, local(): lax.psum((bias_qv_full, fc_full), ('dp', 'wide', 'narrow'))  42.9 us
  transfers between devices with their start and end apart: 19, of which 17 were waited for; matrix products, arithmetic and copies ran while one was open for 6% of the time, Pallas kernels for 0%

commit v1 on v0

--- a/solution.py
+++ b/solution.py
@@ -8,6 +8,29 @@
 HEAD = 64
 EPS = 1e-05
 GELU_C = math.sqrt(2.0 / math.pi)
+
+
+def read_the_tiles(x_local, k_dim):
+    moved = list(x_local.shape[1:])
+    moved[k_dim] *= x_local.shape[0]
+    return jnp.moveaxis(x_local, 0, k_dim).reshape(moved)
+
+
+def _test_ways(incoming_x, a_name):
+    k_all = lax.axis_size(a_name)
+    v1 = incoming_x[None]
+    for tick in range(k_all.bit_length() - 1):
+        field_out = 1 << tick
+        mat_out = lax.ppermute(v1, a_name, [(it, it ^ field_out) for it in range(k_all)])
+        y = jnp.stack([v1, mat_out], axis=0)
+        left_arr = lax.axis_index(a_name) >> tick & 1
+        v1 = jnp.where(left_arr == 0, y, y[::-1]).reshape(-1, *incoming_x.shape)
+    return v1
+
+
+def pack_the_weights(here_x, local_x, d_out):
+    arr_out = _test_ways(here_x, local_x)
+    return read_the_tiles(arr_out, d_out)
 
 
 def gelu_value(pre_act):
@@ -68,9 +91,7 @@
 def project_wide(activations, weight_bf):
     return sum_narrow(
         jnp.dot(
-            lax.all_gather(activations, "wide", axis=0, tiled=True),
-            weight_bf,
-            preferred_element_type=jnp.float32,
+            pack_the_weights(activations, "wide", 0), weight_bf, preferred_element_type=jnp.float32
         )
     )
 

time: 1340 us -> 1420 us (1.060)
  waiting for transfers between devices: 964 us -> 1010 us
  local copies, waits for them, and re-layouts: 37.6 us -> 52.7 us
    ppermute x0 -> x4, waiting for transfers between devices: none -> 96.4 us  [_test_ways(): lax.ppermute(v1, a_name, [(it, it ^ field_out) for it in range(k_all)])]
    reduce_scatter x4, waiting for transfers between devices: 170 us -> 115 us  [sum_narrow(): lax.psum_scatter(partial_value, 'narrow', scatter_dimension=0, tiled=True)]
    all_gather x2, waiting for transfers between devices: 128 us -> 144 us  [fold_wide(): block_rows = lax.all_gather(grad_rows, 'wide', axis=0, tiled=True)]
  transfers between devices with their start and end apart: 19 -> 23, of which waited for: 17 -> 21; matrix products, arithmetic and copies ran while one was open for 6% -> 8% of each run, Pallas kernels for 0% -> 0%
where the time goes in v1:
time: 1420 us
  waiting for transfers between devices  1010 us (71%)
  blocking collectives  165 us (12%)
  matrix products  105 us (7%)
  other arithmetic  53.6 us (4%)
  local copies, waits for them, and re-layouts  52.7 us (4%)
  starting transfers between devices  17.3 us (1%)
  between operations  14.8 us (1%)
    reduce_scatter x4, waiting for transfers between devices, sum_wide(): lax.psum_scatter(partial_rows(), 'wide', scatter_dimension=0, tiled=True)  384 us
    all_gather x2, waiting for transfers between devices, fold_wide(): block_rows = lax.all_gather(grad_rows, 'wide', axis=0, tiled=True)  144 us
    all_gather x4, waiting for transfers between devices, gather_narrow(): return lax.all_gather(values, 'narrow', axis=0, tiled=True)  129 us
    reduce_scatter x4, waiting for transfers between devices, sum_narrow(): lax.psum_scatter(partial_value, 'narrow', scatter_dimension=0, tiled=True)  115 us
    ppermute x4, waiting for transfers between devices, _test_ways(): lax.ppermute(v1, a_name, [(it, it ^ field_out) for it in range(k_all)])  96.4 us
    all_gather x2, waiting for transfers between devices, weight_grad_block(): lax.all_gather(activations, 'wide', axis=0, tiled=True)  82.5 us
    all_to_all x2, waiting for transfers between devices, to_heads(): lax.all_to_all(values, 'narrow', split_axis=0, concat_axis=2, tiled=True)  57.3 us
    all_to_all x2, blocking collectives, from_heads(): lax.all_to_all(values, 'narrow', split_axis=2, concat_axis=0, tiled=True)  54.5 us
  transfers between devices with their start and end apart: 23, of which 21 were waited for; matrix products, arithmetic and copies ran while one was open for 8% of the time, Pallas kernels for 0%

profile of v1, /device:TPU:0, one launch (start us, length us, event | category | flops | bytes accessed | tf_op | source)
XLA Modules:
  0.0 1419.7 jit_solution(283676790046007548)
XLA Ops:
  9.8 11.4 all-reduce.5
  25.0 34.8 %all-gather.9.cloned.1.call-done = bf16[2048,400]{0,1:T(8,128)(2,1)} async-done(((bf16[512,400]{0,1:T(8,128)(2,1)}), bf16[2048,400]{0,1:T(8,128)(2,1)}) %all-gather.9.cloned.1.call-update) | async-done | bytes 1638416 | tf_op jit(solution)/shard_map/all_gather | solution.py:72
  67.2 96.4 %reduce-scatter.9.cloned.1.call-done = f32[512,1200]{0,1:T(8,128)} async-done(((f32[2048,1200]{0,1:T(8,128)}), f32[512,1200]{0,1:T(8,128)}) %reduce-scatter.9.cloned.1.call-update) | async-done | bytes 2457616 | tf_op jit(solution)/shard_map/reduce_scatter | solution.py:88
  173.5 47.8 %all-to-all-done = bf16[512,3,400]{2,1,0:T(4,128)(2,1)S(1)} async-done(((bf16[512,3,400]{2,1,0:T(4,128)(2,1)}), bf16[512,3,400]{2,1,0:T(4,128)(2,1)S(1)}, u32[]{:S(2)}, u32[]{:S(2)}) %all-to-all-start) | async-done | bytes 1228832 | tf_op jit(solution)/shard_map/all_to_all | solution.py:121
  234.3 9.1 reduce.2
  243.5 14.2 all_to_all.63
  271.3 16.7 %collective-permute-done.1 = bf16[2,512,400]{1,2,0:T(8,128)(2,1)S(1)} collective-permute-done((bf16[2,512,400]{1,2,0:T(8,128)(2,1)}, bf16[2,512,400]{1,2,0:T(8,128)(2,1)S(1)}, u32[]{:S(2)}, u32[]{:S(2)}) %collective-permute-start.1) | collective-permute-done | bytes 819232 | tf_op jit(solution)/shard_map/ppermute | solution.py:24
  298.5 59.8 %reduce-scatter.11.cloned.1.call-done = f32[512,400]{0,1:T(8,128)} async-done(((f32[2048,400]{0,1:T(8,128)}), f32[512,400]{0,1:T(8,128)}) %reduce-scatter.11.cloned.1.call-update) | async-done | bytes 819216 | tf_op jit(solution)/shard_map/reduce_scatter | solution.py:76
  359.6 9.9 all-reduce.4
  370.5 27.9 %all-gather.13.cloned.1.call-done = bf16[2048,400]{0,1:T(8,128)(2,1)} async-done(((bf16[512,400]{0,1:T(8,128)(2,1)}), bf16[2048,400]{0,1:T(8,128)(2,1)}) %all-gather.13.cloned.1.call-update) | async-done | bytes 1638416 | tf_op jit(solution)/shard_map/all_gather | solution.py:72
  398.4 10.6 fusion.36
  409.3 28.0 %all-gather.11.cloned.1.call-done = bf16[2048,400]{0,1:T(8,128)(2,1)} async-done(((bf16[512,400]{0,1:T(8,128)(2,1)}), bf16[2048,400]{0,1:T(8,128)(2,1)}) %all-gather.11.cloned.1.call-update) | async-done | bytes 1638416 | tf_op jit(solution)/shard_map/all_gather | solution.py:72
  437.4 11.3 fusion.42
  448.7 115.4 %reduce-scatter.17.cloned.1.call-done = f32[512,1600]{0,1:T(8,128)} async-done(((f32[2048,1600]{0,1:T(8,128)}), f32[512,1600]{0,1:T(8,128)}) %reduce-scatter.17.cloned.1.call-update) | async-done | bytes 3276816 | tf_op jit(solution)/shard_map/reduce_scatter | solution.py:88
  564.1 128.0 %reduce-scatter.13.cloned.1.call-done = f32[512,1600]{0,1:T(8,128)} async-done(((f32[2048,1600]{0,1:T(8,128)}), f32[512,1600]{0,1:T(8,128)}) %reduce-scatter.13.cloned.1.call-update) | async-done | bytes 3276816 | tf_op jit(solution)/shard_map/reduce_scatter | solution.py:88
  699.5 88.8 %all-gather.15.cloned.1.call-done = bf16[2048,1600]{0,1:T(8,128)(2,1)} async-done(((bf16[512,1600]{0,1:T(8,128)(2,1)}), bf16[2048,1600]{0,1:T(8,128)(2,1)}) %all-gather.15.cloned.1.call-update) | async-done | bytes 6553616 | tf_op jit(solution)/shard_map/all_gather | solution.py:100
  788.3 8.5 fusion.40
  801.5 71.2 %collective-permute-done.3 = bf16[2,512,1600]{1,2,0:T(8,128)(2,1)S(1)} collective-permute-done((bf16[2,512,1600]{1,2,0:T(8,128)(2,1)S(1)}, bf16[2,512,1600]{1,2,0:T(8,128)(2,1)S(1)}, u32[]{:S(2)}, u32[]{:S(2)}) %collective-permute-start.3) | collective-permute-done | bytes 3276832 | tf_op jit(solution)/shard_map/ppermute | solution.py:24
  877.5 9.8 copy.163
  897.6 9.1 all-reduce.3
  906.7 51.9 %reduce-scatter.15.cloned.1.call-done = f32[512,400]{0,1:T(8,128)} async-done(((f32[2048,400]{0,1:T(8,128)}), f32[512,400]{0,1:T(8,128)}) %reduce-scatter.15.cloned.1.call-update) | async-done | bytes 819216 | tf_op jit(solution)/shard_map/reduce_scatter | solution.py:76
  962.7 38.2 %all-gather.17.cloned.1.call-done = bf16[2048,400]{0,1:T(8,128)(2,1)} async-done(((bf16[512,400]{0,1:T(8,128)(2,1)}), bf16[2048,400]{0,1:T(8,128)(2,1)}) %all-gather.17.cloned.1.call-update) | async-done | bytes 1638416 | tf_op jit(solution)/shard_map/all_gather | solution.py:72
  1005.0 44.0 %reduce-scatter.21.cloned.1.call-done = f32[512,400]{0,1:T(8,128)} async-done(((f32[2048,400]{0,1:T(8,128)}), f32[512,400]{0,1:T(8,128)}) %reduce-scatter.21.cloned.1.call-update) | async-done | bytes 819216 | tf_op jit(solution)/shard_map/reduce_scatter | solution.py:88
  1061.8 9.5 all-to-all-done.2
  1090.7 40.4 %all_to_all.64 = bf16[128,3,1600]{0,1,2:T(4,128)(2,1)S(1)} all-to-all(bf16[128,3,1600]{0,1,2:T(4,128)(2,1)S(1)} %fusion.11), channel_id=1, replica_groups=mesh['dp'=2,'wide'=4,'narrow'=4] {'narrow'}, dimensions={2} | all-to-all | bytes 2457600 | tf_op jit(solution)/shard_map/all_to_all | solution.py:125
  1134.9 54.9 %all-gather.19.cloned.1.call-done = bf16[2048,1200]{0,1:T(8,128)(2,1)} async-done(((bf16[512,1200]{0,1:T(8,128)(2,1)}), bf16[2048,1200]{0,1:T(8,128)(2,1)}) %all-gather.19.cloned.1.call-update) | async-done | bytes 4915216 | tf_op jit(solution)/shard_map/all_gather | solution.py:100
  1196.8 9.2 fusion.92
  1206.0 57.5 %all-gather.23.cloned.1.call-done = bf16[2048,1600]{0,1:T(8,128)(2,1)} async-done(((bf16[512,1600]{0,1:T(8,128)(2,1)}), bf16[2048,1600]{0,1:T(8,128)(2,1)}) %all-gather.23.cloned.1.call-update) | async-done | bytes 6553616 | tf_op jit(solution)/shard_map/all_gather | solution.py:113
  1271.5 25.0 %all-gather.21.cloned.1.call-done = bf16[2048,400]{0,1:T(8,128)(2,1)} async-done(((bf16[512,400]{0,1:T(8,128)(2,1)}), bf16[2048,400]{0,1:T(8,128)(2,1)}) %all-gather.21.cloned.1.call-update) | async-done | bytes 1638416 | tf_op jit(solution)/shard_map/all_gather | solution.py:113
  1313.8 43.8 %all-reduce = (f32[2,1600]{1,0:T(2,128)S(1)}, f32[6400]{0:T(1024)S(1)}) all-reduce(f32[2,1600]{1,0:T(2,128)S(1)} %pad_maximum_fusion.5, f32[6400]{0:T(1024)S(1)} %dynamic_update_slice.3), channel_id=1, replica_groups=mesh['dp'=2,'wide'=4,'narrow'=4] {'dp','wide','narrow'}, use_global_device_ids=true, to_apply=%region_32.33 | all-reduce | flops 9600 | bytes 76800 | tf_op jit(solution)/shard_map/psum | solution.py:254
  1363.7 9.8 all-reduce.2
  1373.5 27.0 %all-reduce.1 = (f32[400]{0:T(512)}, f32[400]{0:T(512)}, f32[400]{0:T(512)}, f32[400]{0:T(512)}, f32[400]{0:T(512)}, /*index=5*/f32[400]{0:T(512)}) all-reduce(f32[400]{0:T(512)S(1)} %get-tuple-element.114, f32[400]{0:T(512)S(1)} %get-tuple-element.119, ...), channel_id=1, replica_groups=mesh['dp'=2,'wide'=4,'narrow'=4] {'dp','narrow'}, use_global_device_ids=true, to_apply=%region_27.28 | all-reduce | flops 2400 | bytes 19200 | tf_op jit(solution)/shard_map/psum | solution.py:266
  (201 shorter events, 185.0 us)
Async XLA Ops:
  7.2 52.6 %all-gather.9.cloned.1.call-start = ((), (), s32[]{:S(2)}) async-start(), calls=%async_computation.12 | async-start | bytes 2048000 | tf_op jit(solution)/shard_map/all_gather | solution.py:72
  22.2 141.4 %reduce-scatter.9.cloned.1.call-start = ((), (), s32[]{:S(2)}) async-start(), calls=%async_computation.13 | async-start | bytes 12288000 | tf_op jit(solution)/shard_map/reduce_scatter | solution.py:88
  24.9 41.5 %copy-start.22 = (bf16[400,3,400]{0,2,1:T(8,128)(2,1)}, bf16[400,3,400]{0,2,1:T(8,128)(2,1)S(1)}, u32[]{:S(2)}) copy-start(bf16[400,3,400]{0,2,1:T(8,128)(2,1)S(1)} %copy.155) | copy-start | bytes 2880004
  168.5 52.7 %all-to-all-start = ((bf16[512,3,400]{2,1,0:T(4,128)(2,1)}), bf16[512,3,400]{2,1,0:T(4,128)(2,1)S(1)}, u32[]{:S(2)}, u32[]{:S(2)}) async-start(bf16[512,3,400]{2,1,0:T(4,128)(2,1)} %copy.156), calls=%async_computation.1 | async-start | bytes 4194304 | tf_op jit(solution)/shard_map/all_to_all | solution.py:121
  173.2 185.1 %reduce-scatter.11.cloned.1.call-start = ((), (), s32[]{:S(2)}) async-start(), calls=%async_computation.14 | async-start | bytes 4096000 | tf_op jit(solution)/shard_map/reduce_scatter | solution.py:76
  258.5 10.2 collective-permute-start
  269.8 18.2 %collective-permute-start.1 = (bf16[2,512,400]{1,2,0:T(8,128)(2,1)}, bf16[2,512,400]{1,2,0:T(8,128)(2,1)S(1)}, u32[]{:S(2)}, u32[]{:S(2)}) collective-permute-start(bf16[2,512,400]{1,2,0:T(8,128)(2,1)} %get-tuple-element.159), channel_id=1, source_target_pairs={{0,8},{4,12},{8,0},{12,4},{1,9},{5,13},{9,1},{13,5},{2,10},{6,14},... | collective-permute-start | bytes 2457608 | tf_op jit(solution)/shard_map/ppermute | solution.py:24
  296.5 61.8 %copy-start.33 = (f32[400]{0:T(512)S(1)}, f32[400]{0:T(512)}, u32[]{:S(2)}) copy-start(f32[400]{0:T(512)} %param.23) | copy-start | bytes 4804
  296.5 101.9 %all-gather.13.cloned.1.call-start = ((), (), s32[]{:S(2)}) async-start(), calls=%async_computation.18 | async-start | bytes 2048000 | tf_op jit(solution)/shard_map/all_gather | solution.py:72
  298.4 71.1 %copy-start.24 = (f32[400]{0:T(512)S(1)}, f32[400]{0:T(512)}, u32[]{:S(2)}) copy-start(f32[400]{0:T(512)} %param.24) | copy-start | bytes 4804
  298.4 71.1 %copy-start.30 = (f32[400]{0:T(512)S(1)}, f32[400]{0:T(512)}, u32[]{:S(2)}) copy-start(f32[400]{0:T(512)} %param.25) | copy-start | bytes 4804
  298.4 139.0 %all-gather.11.cloned.1.call-start = ((), (), s32[]{:S(2)}) async-start(), calls=%async_computation.15 | async-start | bytes 2048000 | tf_op jit(solution)/shard_map/all_gather | solution.py:72
  370.5 193.6 %reduce-scatter.17.cloned.1.call-start = ((), (), s32[]{:S(2)}) async-start(), calls=%async_computation.19 | async-start | bytes 16384000 | tf_op jit(solution)/shard_map/reduce_scatter | solution.py:88
  409.0 283.1 %reduce-scatter.13.cloned.1.call-start = ((), (), s32[]{:S(2)}) async-start(), calls=%async_computation.16 | async-start | bytes 16384000 | tf_op jit(solution)/shard_map/reduce_scatter | solution.py:88
  448.6 243.5 %copy-start.26 = (f32[1600]{0:T(1024)S(1)}, f32[1600]{0:T(1024)}, u32[]{:S(2)}) copy-start(f32[1600]{0:T(1024)} %param.27) | copy-start | bytes 19204
  448.7 339.6 %all-gather.15.cloned.1.call-start = ((), (), s32[]{:S(2)}) async-start(), calls=%async_computation.20 | async-start | bytes 8192000 | tf_op jit(solution)/shard_map/all_gather | solution.py:100
  697.9 99.5 %copy-start.1 = (bf16[512,1600]{0,1:T(8,128)(2,1)}, bf16[512,1600]{0,1:T(8,128)(2,1)S(1)}, u32[]{:S(2)}) copy-start(bf16[512,1600]{0,1:T(8,128)(2,1)S(1)} %get-tuple-element.147) | copy-start | bytes 4915204
  697.9 198.1 %reduce-scatter.19.cloned.1.call-start = ((), (), s32[]{:S(2)}) async-start(), calls=%async_computation.21 | async-start | bytes 4096000 | tf_op jit(solution)/shard_map/reduce_scatter | solution.py:76
  698.0 99.4 %collective-permute-start.2 = (bf16[1,512,1600]{1,2,0:T(8,128)(2,1)S(1)}, bf16[1,512,1600]{1,2,0:T(8,128)(2,1)}, u32[]{:S(2)}, u32[]{:S(2)}) collective-permute-start(bf16[1,512,1600]{1,2,0:T(8,128)(2,1)S(1)} %bitcast.156), channel_id=1, source_target_pairs={{0,4},{4,0},{8,12},{12,8},{1,5},{5,1},{9,13},{13,9},{2,6},{6,2},{1... | collective-permute-start | bytes 4915208 | tf_op jit(solution)/shard_map/ppermute | solution.py:24
  796.9 161.7 %reduce-scatter.15.cloned.1.call-start = ((), (), s32[]{:S(2)}) async-start(), calls=%async_computation.17 | async-start | bytes 4096000 | tf_op jit(solution)/shard_map/reduce_scatter | solution.py:76
  800.0 72.8 %collective-permute-start.3 = (bf16[2,512,1600]{1,2,0:T(8,128)(2,1)S(1)}, bf16[2,512,1600]{1,2,0:T(8,128)(2,1)S(1)}, u32[]{:S(2)}, u32[]{:S(2)}) collective-permute-start(bf16[2,512,1600]{1,2,0:T(8,128)(2,1)S(1)} %get-tuple-element.149), channel_id=1, source_target_pairs={{0,8},{4,12},{8,0},{12,4},{1,9},{5,13},{9,1},{13,5},{2,10},{6,14},... | collective-permute-start | bytes 9830408 | tf_op jit(solution)/shard_map/ppermute | solution.py:24
  895.9 62.6 %copy-start.8 = (f32[400,512]{1,0:T(8,128)S(1)}, f32[400,512]{1,0:T(8,128)}, u32[]{:S(2)}) copy-start(f32[400,512]{1,0:T(8,128)} %param.16) | copy-start | bytes 2457604
  895.9 62.6 %copy-start.31 = (f32[400]{0:T(512)S(1)}, f32[400]{0:T(512)}, u32[]{:S(2)}) copy-start(f32[400]{0:T(512)} %param.29) | copy-start | bytes 4804
  895.9 104.9 %all-gather.17.cloned.1.call-start = ((), (), s32[]{:S(2)}) async-start(), calls=%async_computation.22 | async-start | bytes 2048000 | tf_op jit(solution)/shard_map/all_gather | solution.py:72
  962.6 86.4 %reduce-scatter.21.cloned.1.call-start = ((), (), s32[]{:S(2)}) async-start(), calls=%async_computation.23 | async-start | bytes 4096000 | tf_op jit(solution)/shard_map/reduce_scatter | solution.py:88
  1054.9 16.5 %all-to-all-start.2 = ((bf16[4,2,25600]{2,1,0:T(2,128)(2,1)}), bf16[4,2,25600]{2,1,0:T(2,128)(2,1)S(1)}, u32[]{:S(2)}, u32[]{:S(2)}) async-start(bf16[4,2,25600]{2,1,0:T(2,128)(2,1)} %reshape.102), calls=%async_computation.9 | async-start | bytes 819200 | tf_op jit(solution)/shard_map/all_to_all | solution.py:121
  1059.5 130.3 %all-gather.19.cloned.1.call-start = ((), (), s32[]{:S(2)}) async-start(), calls=%async_computation.24 | async-start | bytes 6144000 | tf_op jit(solution)/shard_map/all_gather | solution.py:100
  1133.0 130.5 %all-gather.23.cloned.1.call-start = ((), (), s32[]{:S(2)}) async-start(), calls=%async_computation.27 | async-start | bytes 8192000 | tf_op jit(solution)/shard_map/all_gather | solution.py:113
  1133.6 162.9 %all-gather.21.cloned.1.call-start = ((), (), s32[]{:S(2)}) async-start(), calls=%async_computation.26 | async-start | bytes 2048000 | tf_op jit(solution)/shard_map/all_gather | solution.py:113
  1134.9 227.3 %reduce-scatter.23.cloned.1.call-start = ((), (), s32[]{:S(2)}) async-start(), calls=%async_computation.25 | async-start | bytes 4096000 | tf_op jit(solution)/shard_map/reduce_scatter | solution.py:76
  1196.6 207.9 %all-reduce.9.cloned.1.call-start = ((), (), s32[]{:S(2)}) async-start(), calls=%async_computation.28 | async-start | bytes 17203200 | tf_op jit(solution)/shard_map/psum | solution.py:271
  1313.1 60.4 %copy-start.27 = (f32[400]{0:T(512)S(1)}, f32[400]{0:T(512)}, u32[]{:S(2)}) copy-start(f32[400]{0:T(512)} %get-tuple-element.144) | copy-start | bytes 4804
  (26 other events, 187.9 us)
Sparse Core Ops, SparseCore 0:
  22.3 37.4 all-gather.8
  66.6 96.9 reduce-scatter.8
  296.6 61.6 reduce-scatter.10
  360.3 38.0 all-gather.12
  400.4 36.9 all-gather.10
  440.4 123.7 reduce-scatter.16
  567.3 124.8 reduce-scatter.12
  698.0 90.2 all-gather.14
  797.0 62.4 reduce-scatter.18
  896.0 62.4 reduce-scatter.14
  962.7 38.0 all-gather.16
  1005.2 43.8 reduce-scatter.20
  1133.1 56.5 all-gather.18
  1191.4 72.0 all-gather.22
  1265.2 31.2 all-gather.20
  1298.7 63.4 reduce-scatter.22
  1365.9 38.4 all-reduce.8
